TPU v7x, 128 devices: a whole 4x4x4 slice. The times are simulated.
128 devices in a mesh: band: 8 (over x, y_lo), slab: 16 (over z, y_hi, core).
Axes of the slice: x: 4, y: 4 (y_hi: 2, y_lo: 2; y = y_hi * 2 + y_lo), z: 4, core: 2. Of those that a mesh axis runs over, the one named last changes fastest.
Arguments:
- band_fields: float32 [16, 6, 6, 128, 2048], P(None, None, None, ('band', 'slab')), may hold values from -12 to 12
Outputs:
- pair_transfer: float32 [16, 16, 2048], P('band', None, 'slab')
All inputs are finite; a program needn't handle non-finite values.
Results may differ from a plain program's by a relative error of at most 0.0042.
Values may be sent and summed in bfloat16 or wider, within the bound.
A program may use at most 192 MiB of HBM per device.

v0:
```python
import jax
import jax.numpy as jnp
from jax import lax
from jax.sharding import PartitionSpec as P

hall_length = 0.5


def from_behind(array, axis, by):
    peers = lax.axis_size(axis)
    return lax.ppermute(array, axis, [(i, (i + by) % peers) for i in range(peers)])


def advect(vector, ddx, ddy, ddz, first):
    return (
        vector[0] * ddx[:, first : first + 3]
        + vector[1] * ddy[:, first : first + 3]
        + vector[2] * ddz[:, first : first + 3]
    )


def stack_fields(inner, ddx, ddy, ddz):
    currents = jnp.stack([ddy[:, 5] - ddz[:, 4], ddz[:, 3] - ddx[:, 5], ddx[:, 4] - ddy[:, 3]], 1)
    return jnp.concatenate([inner, currents], 1)


def make_drive(inner, ddx, ddy, ddz, full):
    velocity, magnetic, current = (full[0:3], full[3:6], full[6:9])
    part_a = -advect(velocity, ddx, ddy, ddz, 0) + advect(magnetic, ddx, ddy, ddz, 3)
    part_c = -advect(velocity, ddx, ddy, ddz, 3) + advect(magnetic, ddx, ddy, ddz, 0)
    bfield = inner[:, 3:6]
    cross = jnp.stack(
        [
            current[1] * bfield[:, 2] - current[2] * bfield[:, 1],
            current[2] * bfield[:, 0] - current[0] * bfield[:, 2],
            current[0] * bfield[:, 1] - current[1] * bfield[:, 0],
        ],
        1,
    )
    return jnp.concatenate([part_a, part_c, -hall_length * cross], 1).astype(jnp.bfloat16)


def body(band_fields):
    shape_in = band_fields.shape
    opened = band_fields.reshape(
        shape_in[0], shape_in[1], shape_in[2], 1, 1, shape_in[3], shape_in[4]
    )
    received = lax.all_to_all(
        lax.all_to_all(opened, "band", split_axis=0, concat_axis=3, tiled=True),
        "slab",
        split_axis=6,
        concat_axis=4,
        tiled=True,
    )
    shape_got = received.shape
    local = received.reshape(
        shape_got[0],
        shape_got[1],
        shape_got[2],
        shape_got[3] * shape_got[4] * shape_got[5],
        shape_got[6],
    )
    inner = local[:, :, 1:-1]
    ddx = (local[:, :, 2:] - local[:, :, :-2]) * 0.5
    ddy = (jnp.roll(inner, -1, 3) - jnp.roll(inner, 1, 3)) * 0.5
    depth = inner.shape[4]
    from_below = from_behind(inner[:, :, :, :, depth - 1 :], "slab", 1)
    from_above = from_behind(inner[:, :, :, :, 0:1], "slab", -1)
    zindex = lax.broadcasted_iota(jnp.int32, (1, 1, 1, 1, depth), 4)
    upper = jnp.where(zindex == depth - 1, from_above, jnp.roll(inner, -1, 4))
    lower = jnp.where(zindex == 0, from_below, jnp.roll(inner, 1, 4))
    ddz = (upper - lower) * 0.5
    stacked = stack_fields(inner, ddx, ddy, ddz)
    full = lax.psum(jnp.sum(stacked, 0), "band")
    drive = make_drive(inner, ddx, ddy, ddz, full)
    resp = stacked.astype(jnp.bfloat16)
    part = jnp.einsum(
        "qcxyz,kcxyz->qkz",
        resp,
        lax.all_gather(drive, "band", axis=0, tiled=True),
        preferred_element_type=jnp.float32,
    )
    return part * (1.0 / (resp.shape[2] * resp.shape[3]))


def solution(mesh):
    return jax.shard_map(
        body,
        mesh=mesh,
        in_specs=(P(None, None, None, ("band", "slab"), None),),
        out_specs=P("band", None, "slab"),
        check_vma=False,
    )
```

profile of v0, /device:TPU:1, one launch (start us, length us, event | category | flops | bytes accessed | tf_op | source)
XLA Modules:
  0.0 1321.4 jit_solution(17489046539009117229)
XLA Ops:
  6.5 60.1 %all_to_all.27 = f32[16,6,6,1,1,1,2048]{6,3,5,4,2,1,0:T(1,128)S(1)} all-to-all(f32[16,6,6,1,1,1,2048]{6,3,5,4,2,1,0:T(1,128)} %bitcast.48), channel_id=1, replica_groups=mesh['band'=8,'slab'=16] {'band'}, dimensions={0} | all-to-all | bytes 9437184 | tf_op jit(solution)/shard_map/all_to_all | solution.py:49
  66.6 5.5 copy.110
  72.2 88.5 %copy.75 = f32[2,6,6,8,1,1,2048]{3,0,5,4,2,1,6:T(2,128)} copy(f32[2,6,6,8,1,1,2048]{6,3,2,1,0,5,4:T(8,128)} %bitcast.46) | data formatting | bytes 9437184 | tf_op jit(solution)/shard_map/all_to_all | solution.py:49
  160.7 170.6 %reshape.29 = f32[16,1,73728]{2,1,0:T(1,128)} reshape(f32[2048,6,6,1,1,2,8]{6,5,4,3,2,1,0:T(2,128)} %bitcast.40) | data formatting | bytes 9437184
  331.3 9.5 all-to-all-start.1
  340.8 0.5 all-reduce.2.cloned.1.call-start
  341.3 56.0 %all-to-all-done.1 = f32[16,1,73728]{2,1,0:T(1,128)} async-done(((f32[16,1,73728]{2,1,0:T(1,128)}), f32[16,1,73728]{2,1,0:T(1,128)}, u32[]{:S(2)}, u32[]{:S(2)}) %all-to-all-start.1) | async-done | bytes 4718624 | tf_op jit(solution)/shard_map/all_to_all | solution.py:48
  397.3 0.5 broadcast.25
  397.8 16.0 %reduce = f32[16,73728]{1,0:T(8,128)} reduce(f32[16,1,73728]{2,1,0:T(1,128)} %all-to-all-done.1, f32[]{:T(128)} %broadcast.25), dimensions={1}, to_apply=%all_to_all.24.reduce_sub_computation | reduce | bytes 9437188 | tf_op jit(solution)/shard_map/all_to_all | solution.py:48
  413.8 158.9 %reshape.30 = f32[2048,6,6,1,1,2,8]{6,5,4,3,2,1,0:T(2,128)} reshape(f32[16,73728]{1,0:T(8,128)} %reduce) | data formatting | bytes 9437184
  572.7 92.1 %copy.76 = f32[2,6,6,8,1,1,2048]{6,3,2,1,0,5,4:T(8,128)} copy(f32[2,6,6,8,1,1,2048]{3,0,5,4,2,1,6:T(2,128)} %bitcast.41) | data formatting | bytes 9437184 | tf_op jit(solution)/shard_map/all_to_all | solution.py:48
  664.8 5.9 reshape.27
  670.7 6.5 fusion.18
  677.3 0.0 copy-done
  677.3 3.3 fusion.21
  680.6 3.8 fusion.17
  684.4 2.4 copy.100
  686.8 1.3 collective-permute-start
  688.0 2.4 copy.102
  690.4 2.3 collective-permute-start.1
  692.7 5.8 copy.96
  698.5 5.9 copy.99
  704.4 3.6 copy.97
  708.0 3.5 copy.98
  711.5 5.9 copy.104
  717.4 5.9 copy.105
  723.2 6.7 subtract_multiply_fusion
  730.0 0.0 copy-done.5
  730.0 9.5 fusion
  739.5 3.8 fusion.19
  743.3 5.9 copy.101
  749.2 5.9 copy.103
  755.1 3.6 copy.95
  758.7 0.0 collective-permute-done
  758.7 0.0 collective-permute-done.1
  758.7 10.2 fusion.2
  768.9 2.5 slice_subtract_fusion.2
  771.4 0.8 copy-done.7
  772.2 0.2 copy-done.8
  772.4 0.2 copy-done.9
  772.6 9.9 fusion.15
  782.5 0.0 all-reduce.2.cloned.1.call-update
  782.5 0.0 all-gather.2.cloned.1.call-start
  782.6 2.5 fusion.16
  785.1 2.1 copy.106
  787.2 2.1 copy.107
  789.2 2.0 copy.108
  791.3 101.3 %all-reduce.2.cloned.1.call-done = f32[9,4,128,128]{2,1,0,3:T(4,128)} async-done(((f32[9,4,128,128]{2,1,0,3:T(4,128)}), f32[9,4,128,128]{2,1,0,3:T(4,128)}) %all-reduce.2.cloned.1.call-update) | async-done | bytes 2359312 | tf_op jit(solution)/shard_map/psum | solution.py:74
  892.6 1.9 slice_bitcast_fusion.8
  894.5 0.0 copy-done.10
  894.5 0.0 copy-done.11
  894.5 0.2 copy-done.12
  894.7 0.8 multiply_subtract_fusion.2
  895.5 0.9 fusion.5
  896.4 0.2 copy-done.1
  896.6 1.0 copy-done.2
  897.6 8.3 add_convert_fusion.1
  905.9 3.3 pad_maximum_fusion.1
  909.2 4.6 copy.91
  913.8 0.0 all-gather.2.cloned.1.call-update
  913.9 366.2 %all-gather.2.cloned.1.call-done = bf16[16,9,4,128,128]{4,3,2,1,0:T(8,128)(2,1)} async-done(((bf16[2,9,4,128,128]{4,3,2,1,0:T(8,128)(2,1)}), bf16[16,9,4,128,128]{4,3,2,1,0:T(8,128)(2,1)}) %all-gather.2.cloned.1.call-update) | async-done | bytes 18874384 | tf_op jit(solution)/shard_map/all_gather | solution.py:80
  1280.1 24.0 %copy.92 = bf16[16,9,4,128,128]{3,0,2,1,4:T(8,128)(2,1)} copy(bf16[16,9,4,128,128]{4,3,2,1,0:T(8,128)(2,1)} %all-gather.2.cloned.1.call-done) | data formatting | bytes 37748736 | tf_op jit(solution)/shard_map/all_gather | solution.py:80
  1304.1 9.6 fusion.12
  1313.6 0.7 copy.93
  (23 shorter events, 0.1 us)
Async XLA Ops:
  331.3 66.0 %all-to-all-start.1 = ((f32[16,1,73728]{2,1,0:T(1,128)}), f32[16,1,73728]{2,1,0:T(1,128)}, u32[]{:S(2)}, u32[]{:S(2)}) async-start(f32[16,1,73728]{2,1,0:T(1,128)} %reshape.29), calls=%async_computation.1 | async-start | bytes 9437184 | tf_op jit(solution)/shard_map/all_to_all | solution.py:48
  340.8 551.8 %all-reduce.2.cloned.1.call-start = ((), (), s32[]{:S(2)}) async-start(), calls=%async_computation.2 | async-start | bytes 4718592 | tf_op jit(solution)/shard_map/psum | solution.py:74
  670.7 6.5 copy-start
  686.8 71.9 %collective-permute-start = (f32[2,6,4,128,1]{3,0,2,1,4:T(2,128)S(1)}, f32[2,6,4,128,1]{3,0,2,1,4:T(2,128)S(1)}, u32[]{:S(2)}, u32[]{:S(2)}) collective-permute-start(f32[2,6,4,128,1]{3,0,2,1,4:T(2,128)S(1)} %copy.100), channel_id=1, source_target_pairs={{0,15},{1,0},{2,1},{3,2},{4,3},{5,4},{6,5},{7,6},{8,7},{9,8},{10,9... | collective-permute-start | bytes 73736 | tf_op jit(solution)/shard_map/ppermute | solution.py:11
  690.4 68.3 %collective-permute-start.1 = (f32[2,6,4,128,1]{3,0,2,1,4:T(2,128)S(1)}, f32[2,6,4,128,1]{3,0,2,1,4:T(2,128)S(1)}, u32[]{:S(2)}, u32[]{:S(2)}) collective-permute-start(f32[2,6,4,128,1]{3,0,2,1,4:T(2,128)S(1)} %copy.102), channel_id=1, source_target_pairs={{0,1},{1,2},{2,3},{3,4},{4,5},{5,6},{6,7},{7,8},{8,9},{9,10},{10,1... | collective-permute-start | bytes 73736 | tf_op jit(solution)/shard_map/ppermute | solution.py:11
  723.2 6.7 copy-start.5
  723.2 6.7 copy-start.6
  723.2 16.2 %slice-start = ((s8[4718592]{0:T(1024)(128)(4,1)}), s8[524288]{0:T(1024)(128)(4,1)S(1)}, s32[]{:S(2)}) async-start(s8[4718592]{0:T(1024)(128)(4,1)} %bitcast.44), calls=%async_computation.4 | async-start | bytes 1048576
  730.0 9.5 slice-start.1
  768.9 3.8 copy-start.3
  771.4 0.8 copy-start.7
  771.4 1.0 copy-start.8
  771.4 1.2 copy-start.9
  782.5 497.6 %all-gather.2.cloned.1.call-start = ((), (), s32[]{:S(2)}) async-start(), calls=%async_computation.3 | async-start | bytes 21233664 | tf_op jit(solution)/shard_map/all_gather | solution.py:80
  892.6 1.9 copy-start.10
  892.6 2.0 copy-start.11
  892.6 2.1 copy-start.12
  894.7 1.9 copy-start.1
  894.7 2.8 copy-start.2
  913.9 390.2 %copy-start.4 = (f32[2,6,4,128,128]{3,0,2,1,4:T(2,128)S(1)}, f32[2,6,4,128,128]{3,0,2,1,4:T(2,128)}, u32[]{:S(2)}) copy-start(f32[2,6,4,128,128]{3,0,2,1,4:T(2,128)} %copy.95) | copy-start | bytes 9437188
Sparse Core Ops, SparseCore 0:
  782.6 109.8 all-reduce.1
  914.0 366.0 all-gather.1
where the time goes:
time: 1340 us; the launch traced here: 1320 us
  local copies, waits for them, and re-layouts  633 us (47%)
  waiting for transfers between devices  524 us (39%)
  other arithmetic  68.1 us (5%)
  blocking collectives  60.1 us (4%)
  between operations  13.8 us (1%)
  starting transfers between devices  13.6 us (1%)
    unnamed x46, local copies, waits for them, and re-layouts  389 us
    all_gather x1, waiting for transfers between devices, body(): lax.all_gather(drive, 'band', axis=0, tiled=True)  366 us
    psum x1, waiting for transfers between devices, body(): full = lax.psum(jnp.sum(stacked, 0), 'band')  101 us
    all_to_all x2, local copies, waits for them, and re-layouts, body(): lax.all_to_all(opened, 'band', split_axis=0, concat_axis=3, tiled=True)  94.1 us
    all_to_all x2, local copies, waits for them, and re-layouts, body(): lax.all_to_all(lax.all_to_all(opened, 'band', split_axis=0, concat_axis=3...  92.6 us
    all_to_all x1, blocking collectives, body(): lax.all_to_all(opened, 'band', split_axis=0, concat_axis=3, tiled=True)  60.1 us
    all_to_all x1, waiting for transfers between devices, body(): lax.all_to_all(lax.all_to_all(opened, 'band', split_axis=0, concat_axis=3...  56 us
  transfers between devices with their start and end apart: 5, of which 3 were waited for; matrix products, arithmetic and copies ran while one was open for 6% of the time, Pallas kernels for 0%

commit v1 on v0

v1 whole, which is shorter than its diff:
```python
import functools

import jax
import jax.numpy as jnp
from jax import lax
from jax.experimental import pallas as pl
from jax.experimental.pallas import tpu as pltpu
from jax.sharding import PartitionSpec as P

MESH = pl.DeviceIdType.MESH
F32 = jnp.float32
BF16 = jnp.bfloat16

STARTS = (0, 6, 12, 19, 25, 31)
SIZES = (6, 6, 7, 6, 6, 6)
EDGE = 18
TILES = 37


def kernel(nb, ns, x_ref, o_ref, xv, edges, send, recv, resp, drive, acc, parts,
           load_sem, own_sem, send_sem, recv_sem, hs_sem, hr_sem, ps_sem, pr_sem):
    band = lax.axis_index("band")
    slab = lax.axis_index("slab")

    load = pltpu.make_async_copy(x_ref, xv, load_sem)
    load.start()

    barrier = pltpu.get_barrier_semaphore()

    def greet_slab(k, carry):
        pl.semaphore_signal(barrier, inc=1, device_id=(band, lax.rem(slab + k, ns)), device_id_type=MESH)
        return carry

    def greet_band(k, carry):
        pl.semaphore_signal(barrier, inc=1, device_id=(lax.rem(band + k, nb), slab), device_id_type=MESH)
        return carry

    lax.fori_loop(1, ns, greet_slab, 0)
    lax.fori_loop(1, nb, greet_band, 0)
    load.wait()

    lane = lax.broadcasted_iota(jnp.int32, (16, 128), 1)
    pair = lane // 2

    def pack(s, carry):
        edge = jnp.zeros((16, 128), F32)
        for x in range(6):
            for c in range(6):
                tile = xv[pl.ds(c * 96 + x * 16 + s, 16, stride=576), :]
                send[s, STARTS[x] + c + (0), :, :] = tile.astype(BF16)
                if 1 <= x <= 4:
                    i = (x - 1) * 6 + c
                    edge = jnp.where(pair == i, pltpu.roll(tile, 2 * i + 1, 1), edge)
        edges[s] = edge
        return carry

    lax.fori_loop(0, ns, pack, 0)

    def pack_edges(s, carry):
        above = pltpu.roll(edges[lax.rem(s + 1, ns)], 127, 1)
        below = pltpu.roll(edges[lax.rem(s + ns - 1, ns)], 1, 1)
        send[s, EDGE] = jnp.where(lane - 2 * pair == 0, above, below).astype(BF16)
        return carry

    lax.fori_loop(0, ns, pack_edges, 0)

    own = pltpu.make_async_copy(send.at[slab], recv.at[slab + 1], own_sem)
    own.start()

    pl.semaphore_wait(barrier, ns - 1 + nb - 1)

    def message(x, k):
        to = lax.rem(slab + k, ns)
        tiles = pl.ds(STARTS[x], SIZES[x])
        return pltpu.make_async_remote_copy(
            src_ref=send.at[to, tiles],
            dst_ref=recv.at[slab + 1, tiles],
            send_sem=send_sem.at[x, k],
            recv_sem=recv_sem.at[x, k],
            device_id=(band, to),
            device_id_type=MESH,
        )

    for x in range(6):
        def start(k, carry, x=x):
            message(x, k).start()
            return carry
        lax.fori_loop(1, ns, start, 0)

    def wait_plane(x):
        def wait(k, carry):
            message(x, k).wait_recv()
            return carry
        lax.fori_loop(1, ns, wait, 0)

    def halo(x, up):
        tiles = pl.ds(STARTS[x], 6)
        return pltpu.make_async_remote_copy(
            src_ref=recv.at[ns if up else 1, tiles],
            dst_ref=recv.at[0 if up else ns + 1, tiles],
            send_sem=hs_sem.at[x - 1, up],
            recv_sem=hr_sem.at[x - 1, up],
            device_id=(lax.rem(band + (1 if up else nb - 1), nb), slab),
            device_id_type=MESH,
        )

    def compute(x):
        lo, mid, hi = STARTS[x - 1], STARTS[x], STARTS[x + 1]

        def fields(y, carry):
            def tile(row, t):
                return recv[row, t].astype(F32)

            edge = tile(y + 1, EDGE)
            inner, dx, dy, dz = [], [], [], []
            for c in range(6):
                value = tile(y + 1, mid + c)
                inner.append(value)
                dx.append(tile(y + 1, hi + c) - tile(y + 1, lo + c))
                dy.append(tile(y + 2, mid + c) - tile(y, mid + c))
                ends = pltpu.roll(edge, 127 - 2 * ((x - 1) * 6 + c), 1)
                upper = jnp.where(lane == 127, ends, pltpu.roll(value, 127, 1))
                lower = jnp.where(lane == 0, ends, pltpu.roll(value, 1, 1))
                dz.append(upper - lower)
            current = [dy[5] - dz[4], dz[3] - dx[5], dx[4] - dy[3]]

            def total(value, scale):
                return jnp.sum(value, axis=0, keepdims=True) * scale

            v = [total(inner[c], -0.5) for c in range(3)]
            b = [total(inner[3 + c], 0.5) for c in range(3)]
            j = [total(current[c], -0.25) for c in range(3)]
            for c in range(6):
                resp[y, c] = inner[c]
            for c in range(3):
                resp[y, 6 + c] = current[c] * 0.5
            for c in range(3):
                e = 3 + c
                drive[y, c] = (v[0] * dx[c] + v[1] * dy[c] + v[2] * dz[c]) + (
                    b[0] * dx[e] + b[1] * dy[e] + b[2] * dz[e])
                drive[y, e] = (v[0] * dx[e] + v[1] * dy[e] + v[2] * dz[e]) + (
                    b[0] * dx[c] + b[1] * dy[c] + b[2] * dz[c])
            drive[y, 6] = j[1] * inner[5] - j[2] * inner[4]
            drive[y, 7] = j[2] * inner[3] - j[0] * inner[5]
            drive[y, 8] = j[0] * inner[4] - j[1] * inner[3]
            return carry

        lax.fori_loop(0, ns, fields, 0)

        def contract(y, sums):
            sums = list(sums)
            for c in range(9):
                d = drive[y, c]
                for q in range(16):
                    sums[q] = sums[q] + resp[y, c, pl.ds(q, 1), :] * d
            return tuple(sums)

        if x == 1:
            first = tuple(jnp.zeros((16, 128), F32) for q in range(16))
        else:
            first = tuple(acc[q] for q in range(16))
        sums = lax.fori_loop(0, ns, contract, first)
        for q in range(16):
            acc[q] = sums[q]

    own.wait()
    wait_plane(0)
    for x in range(1, 6):
        wait_plane(x)
        if x <= 4:
            halo(x, 0).start()
            halo(x, 1).start()
        if x >= 2:
            halo(x - 1, 0).wait_recv()
            halo(x - 1, 1).wait_recv()
            compute(x - 1)

    def part(k):
        to = lax.rem(band + k, nb)
        return pltpu.make_async_remote_copy(
            src_ref=acc.at[pl.ds(2 * to, 2)],
            dst_ref=parts.at[k - 1],
            send_sem=ps_sem.at[k - 1],
            recv_sem=pr_sem.at[k - 1],
            device_id=(to, slab),
            device_id_type=MESH,
        )

    for k in range(1, nb):
        part(k).start()
    result = acc[pl.ds(2 * band, 2)]
    for k in range(1, nb):
        part(k).wait_recv()
        result = result + parts[k - 1]
    o_ref[...] = result * (1.0 / 512.0)

    for x in range(6):
        def drain(k, carry, x=x):
            message(x, k).wait_send()
            return carry
        lax.fori_loop(1, ns, drain, 0)
    for x in range(1, 5):
        halo(x, 0).wait_send()
        halo(x, 1).wait_send()
    for k in range(1, nb):
        part(k).wait_send()


def body(band_fields):
    nb, ns = lax.axis_size("band"), lax.axis_size("slab")
    rows = band_fields.reshape(16 * 36 * 16, 128)
    dma = pltpu.SemaphoreType.DMA
    return pl.pallas_call(
        functools.partial(kernel, nb, ns),
        out_shape=jax.ShapeDtypeStruct((2, 16, 128), F32),
        in_specs=[pl.BlockSpec(memory_space=pltpu.HBM)],
        out_specs=pl.BlockSpec(memory_space=pltpu.VMEM),
        scratch_shapes=[
            pltpu.VMEM((9216, 128), F32),
            pltpu.VMEM((ns, 16, 128), F32),
            pltpu.VMEM((ns, TILES, 16, 128), BF16),
            pltpu.VMEM((ns + 2, TILES, 16, 128), BF16),
            pltpu.VMEM((ns, 9, 16, 128), F32),
            pltpu.VMEM((ns, 9, 16, 128), F32),
            pltpu.VMEM((16, 16, 128), F32),
            pltpu.VMEM((nb - 1, 2, 16, 128), F32),
            dma,
            dma,
            dma((6, ns)),
            dma((6, ns)),
            dma((4, 2)),
            dma((4, 2)),
            dma((nb - 1,)),
            dma((nb - 1,)),
        ],
        compiler_params=pltpu.CompilerParams(
            collective_id=0, has_side_effects=True, vmem_limit_bytes=48 << 20
        ),
    )(rows)


def solution(mesh):
    return jax.shard_map(
        body,
        mesh=mesh,
        in_specs=(P(None, None, None, ("band", "slab"), None),),
        out_specs=P("band", None, "slab"),
        check_vma=False,
    )
```

time: 1340 us -> 60.8 us (0.05); the launches traced: 1320 us -> 59.7 us
  local copies, waits for them, and re-layouts: 633 us -> 2.94 us
  waiting for transfers between devices: 524 us -> 0 us
  other arithmetic: 68.1 us -> 0 us
  blocking collectives: 60.1 us -> 0 us
  Pallas kernels: 0 us -> 56.7 us
  between operations: 13.8 us -> 0.01 us
  starting transfers between devices: 13.6 us -> 0 us
    unnamed x46 -> x3, local copies, waits for them, and re-layouts: 389 us -> 2.94 us
    all_gather x1 -> x0, waiting for transfers between devices: 366 us -> none  [body(): lax.all_gather(drive, 'band', axis=0, tiled=True)]
    all_to_all x4 -> x0, local copies, waits for them, and re-layouts: 187 us -> none  [the longest x2 94.1 us: body(): lax.all_to_all(opened, 'band', split_axis=0, concat_axis=3, tiled=True)]
    psum x1 -> x0, waiting for transfers between devices: 101 us -> none  [body(): full = lax.psum(jnp.sum(stacked, 0), 'band')]
    all_to_all x1 -> x0, blocking collectives: 60.1 us -> none  [body(): lax.all_to_all(opened, 'band', split_axis=0, concat_axis=3, tiled=True)]
    pallas_call x0 -> x1, Pallas kernels: none -> 56.7 us  [body(): pl.pallas_call(functools.partial(kernel, nb, ns), out_shape=jax.ShapeDtyp...]
    all_to_all x1 -> x0, waiting for transfers between devices: 56 us -> none  [body(): lax.all_to_all(lax.all_to_all(opened, 'band', split_axis=0, concat_axis=3...]
    mul x3 -> x0, other arithmetic: 26.4 us -> none  [the longest x1 10.2 us: body(): ddz = (upper - lower) * 0.5]
  transfers between devices with their start and end apart: 5 -> 0, of which waited for: 3 -> 0; matrix products, arithmetic and copies ran while one was open for 6% -> 0% of each run, Pallas kernels for 0% -> 0%
where the time goes in v1:
time: 60.8 us; the launch traced here: 59.7 us
  Pallas kernels  56.7 us (93%)
  local copies, waits for them, and re-layouts  2.94 us (5%)
    pallas_call x1, Pallas kernels, body(): pl.pallas_call(functools.partial(kernel, nb, ns), out_shape=jax.ShapeDtyp...  56.7 us
    unnamed x3, local copies, waits for them, and re-layouts  2.94 us

profile of v1, /device:TPU:1, one launch (start us, length us, event | category | flops | bytes accessed | tf_op | source)
XLA Modules:
  0.0 59.7 jit_solution(7662766156652180953)
XLA Ops:
  0.0 0.0 copy-start
  0.0 2.3 %copy-done = f32[16,6,6,1,2048]{4,3,2,1,0:T(1,128)S(1)} copy-done((f32[16,6,6,1,2048]{4,3,2,1,0:T(1,128)S(1)}, f32[16,6,6,1,2048]{4,3,2,1,0:T(1,128)}, u32[]{:S(2)}) %copy-start) | copy-done | bytes 4718616
  2.3 56.7 %shard_map.17 = f32[2,16,128]{2,1,0:T(8,128)S(1)} custom-call(f32[9216,128]{1,0:T(8,128)S(1)} %bitcast.1), custom_call_target="tpu_custom_call" | custom-call | tf_op jit(solution)/shard_map/pallas_call | solution.py:213
  59.1 0.6 %copy.3 = f32[2,16,128]{2,1,0:T(8,128)} copy(f32[2,16,128]{2,1,0:T(8,128)S(1)} %shard_map.17) | data formatting | bytes 32768
Async XLA Ops:
  0.0 2.3 %copy-start = (f32[16,6,6,1,2048]{4,3,2,1,0:T(1,128)S(1)}, f32[16,6,6,1,2048]{4,3,2,1,0:T(1,128)}, u32[]{:S(2)}) copy-start(f32[16,6,6,1,2048]{4,3,2,1,0:T(1,128)} %param.1) | copy-start | bytes 14155780

commit v2 on v1

--- a/solution.py
+++ b/solution.py
@@ -11,8 +11,8 @@
 F32 = jnp.float32
 BF16 = jnp.bfloat16
 
-STARTS = (0, 6, 12, 19, 25, 31)
-SIZES = (6, 6, 7, 6, 6, 6)
+STARTS = (25, 0, 6, 12, 19, 31)
+SIZES = (6, 6, 6, 7, 6, 6)
 EDGE = 18
 TILES = 37
 
@@ -22,8 +22,8 @@
     band = lax.axis_index("band")
     slab = lax.axis_index("slab")
 
-    load = pltpu.make_async_copy(x_ref, xv, load_sem)
-    load.start()
+    def load(x):
+        return pltpu.make_async_copy(x_ref.at[:, x], xv.at[x], load_sem.at[x])
 
     barrier = pltpu.get_barrier_semaphore()
 
@@ -37,24 +37,30 @@
 
     lax.fori_loop(1, ns, greet_slab, 0)
     lax.fori_loop(1, nb, greet_band, 0)
-    load.wait()
+    for x in range(6):
+        load(x).start()
 
     lane = lax.broadcasted_iota(jnp.int32, (16, 128), 1)
     pair = lane // 2
-
-    def pack(s, carry):
-        edge = jnp.zeros((16, 128), F32)
-        for x in range(6):
+    rows = xv.reshape(6 * 96 * 16, 128)
+
+    def pack(x):
+        load(x).wait()
+
+        def step(s, carry):
+            if 1 <= x <= 4:
+                edge = jnp.zeros((16, 128), F32) if x == 1 else edges[s]
             for c in range(6):
-                tile = xv[pl.ds(c * 96 + x * 16 + s, 16, stride=576), :]
-                send[s, STARTS[x] + c + (0), :, :] = tile.astype(BF16)
+                tile = rows[pl.ds(x * 1536 + c * 16 + s, 16, stride=96), :]
+                send[s, STARTS[x] + c] = tile.astype(BF16)
                 if 1 <= x <= 4:
                     i = (x - 1) * 6 + c
                     edge = jnp.where(pair == i, pltpu.roll(tile, 2 * i + 1, 1), edge)
-        edges[s] = edge
-        return carry
-
-    lax.fori_loop(0, ns, pack, 0)
+            if 1 <= x <= 4:
+                edges[s] = edge
+            return carry
+
+        lax.fori_loop(0, ns, step, 0)
 
     def pack_edges(s, carry):
         above = pltpu.roll(edges[lax.rem(s + 1, ns)], 127, 1)
@@ -62,12 +68,7 @@
         send[s, EDGE] = jnp.where(lane - 2 * pair == 0, above, below).astype(BF16)
         return carry
 
-    lax.fori_loop(0, ns, pack_edges, 0)
-
     own = pltpu.make_async_copy(send.at[slab], recv.at[slab + 1], own_sem)
-    own.start()
-
-    pl.semaphore_wait(barrier, ns - 1 + nb - 1)
 
     def message(x, k):
         to = lax.rem(slab + k, ns)
@@ -81,11 +82,17 @@
             device_id_type=MESH,
         )
 
-    for x in range(6):
-        def start(k, carry, x=x):
+    def start_plane(x):
+        def start(k, carry):
             message(x, k).start()
             return carry
         lax.fori_loop(1, ns, start, 0)
+
+    def drain_plane(x):
+        def drain(k, carry):
+            message(x, k).wait_send()
+            return carry
+        lax.fori_loop(1, ns, drain, 0)
 
     def wait_plane(x):
         def wait(k, carry):
@@ -145,7 +152,10 @@
             drive[y, 8] = j[0] * inner[4] - j[1] * inner[3]
             return carry
 
-        lax.fori_loop(0, ns, fields, 0)
+        lax.fori_loop(1, ns - 1, fields, 0)
+        halo(x, 0).wait_recv()
+        halo(x, 1).wait_recv()
+        lax.fori_loop(0, 2, lambda i, carry: fields(i * (ns - 1), carry), 0)
 
         def contract(y, sums):
             sums = list(sums)
@@ -155,25 +165,15 @@
                     sums[q] = sums[q] + resp[y, c, pl.ds(q, 1), :] * d
             return tuple(sums)
 
-        if x == 1:
+        if x == 4:
+            return
+        if x == 2:
             first = tuple(jnp.zeros((16, 128), F32) for q in range(16))
         else:
             first = tuple(acc[q] for q in range(16))
         sums = lax.fori_loop(0, ns, contract, first)
         for q in range(16):
             acc[q] = sums[q]
-
-    own.wait()
-    wait_plane(0)
-    for x in range(1, 6):
-        wait_plane(x)
-        if x <= 4:
-            halo(x, 0).start()
-            halo(x, 1).start()
-        if x >= 2:
-            halo(x - 1, 0).wait_recv()
-            halo(x - 1, 1).wait_recv()
-            compute(x - 1)
 
     def part(k):
         to = lax.rem(band + k, nb)
@@ -186,19 +186,70 @@
             device_id_type=MESH,
         )
 
-    for k in range(1, nb):
-        part(k).start()
+    def finish(steps):
+        groups = [2 * lax.rem(band + k, nb) + r for k in steps for r in range(2)]
+
+        def contract(y, sums):
+            sums = list(sums)
+            for c in range(9):
+                d = drive[y, c]
+                for i, q in enumerate(groups):
+                    sums[i] = sums[i] + resp[y, c, pl.ds(q, 1), :] * d
+            return tuple(sums)
+
+        sums = lax.fori_loop(0, ns, contract, tuple(acc[q] for q in groups))
+        for i, q in enumerate(groups):
+            acc[q] = sums[i]
+        for k in steps:
+            if k:
+                part(k).start()
+
+    pack(1)
+    pack(2)
+    pl.semaphore_wait(barrier, ns - 1 + nb - 1)
+    start_plane(1)
+    start_plane(2)
+    for x in (3, 4, 0, 5):
+        pack(x)
+    lax.fori_loop(0, ns, pack_edges, 0)
+    own.start()
+    drain_plane(1)
+    start_plane(3)
+    drain_plane(2)
+    start_plane(4)
+    own.wait()
+
+    def arrive(x):
+        wait_plane(x)
+        if 1 <= x <= 4:
+            halo(x, 0).start()
+            halo(x, 1).start()
+
+    arrive(1)
+    arrive(2)
+    arrive(3)
+    drain_plane(3)
+    start_plane(0)
+    compute(2)
+    arrive(4)
+    drain_plane(4)
+    start_plane(5)
+    compute(3)
+    arrive(0)
+    compute(1)
+    arrive(5)
+    compute(4)
+    for steps in ((4, 5), (3, 2), (6, 7), (1, 0)):
+        finish(steps)
+
     result = acc[pl.ds(2 * band, 2)]
     for k in range(1, nb):
         part(k).wait_recv()
         result = result + parts[k - 1]
     o_ref[...] = result * (1.0 / 512.0)
 
-    for x in range(6):
-        def drain(k, carry, x=x):
-            message(x, k).wait_send()
-            return carry
-        lax.fori_loop(1, ns, drain, 0)
+    for x in (0, 5):
+        drain_plane(x)
     for x in range(1, 5):
         halo(x, 0).wait_send()
         halo(x, 1).wait_send()
@@ -208,7 +259,7 @@
 
 def body(band_fields):
     nb, ns = lax.axis_size("band"), lax.axis_size("slab")
-    rows = band_fields.reshape(16 * 36 * 16, 128)
+    rows = band_fields.reshape(96, 6, 16, 128)
     dma = pltpu.SemaphoreType.DMA
     return pl.pallas_call(
         functools.partial(kernel, nb, ns),
@@ -216,7 +267,7 @@
         in_specs=[pl.BlockSpec(memory_space=pltpu.HBM)],
         out_specs=pl.BlockSpec(memory_space=pltpu.VMEM),
         scratch_shapes=[
-            pltpu.VMEM((9216, 128), F32),
+            pltpu.VMEM((6, 96, 16, 128), F32),
             pltpu.VMEM((ns, 16, 128), F32),
             pltpu.VMEM((ns, TILES, 16, 128), BF16),
             pltpu.VMEM((ns + 2, TILES, 16, 128), BF16),
@@ -224,7 +275,7 @@
             pltpu.VMEM((ns, 9, 16, 128), F32),
             pltpu.VMEM((16, 16, 128), F32),
             pltpu.VMEM((nb - 1, 2, 16, 128), F32),
-            dma,
+            dma((6,)),
             dma,
             dma((6, ns)),
             dma((6, ns)),
@@ -234,7 +285,7 @@
             dma((nb - 1,)),
         ],
         compiler_params=pltpu.CompilerParams(
-            collective_id=0, has_side_effects=True, vmem_limit_bytes=48 << 20
+            collective_id=0, has_side_effects=True, vmem_limit_bytes=62 << 20
         ),
     )(rows)
 

time: 60.8 us -> 53.5 us (0.88); the launches traced: 59.7 us -> 53.3 us
  Pallas kernels: 56.7 us -> 52 us
  local copies, waits for them, and re-layouts: 2.94 us -> 1.32 us
    pallas_call x1, Pallas kernels: 56.7 us -> 52 us  [body(): pl.pallas_call(functools.partial(kernel, nb, ns), out_shape=jax.ShapeDtyp...]
    unnamed x3 -> x1, local copies, waits for them, and re-layouts: 2.94 us -> 1.32 us
where the time goes in v2:
time: 53.5 us; the launch traced here: 53.3 us
  Pallas kernels  52 us (97%)
  local copies, waits for them, and re-layouts  1.32 us (2%)
    pallas_call x1, Pallas kernels, body(): pl.pallas_call(functools.partial(kernel, nb, ns), out_shape=jax.ShapeDtyp...  52 us
    unnamed x1, local copies, waits for them, and re-layouts  1.32 us

profile of v2, /device:TPU:1, one launch (start us, length us, event | category | flops | bytes accessed | tf_op | source)
XLA Modules:
  0.0 53.3 jit_solution(13832066896083557828)
XLA Ops:
  0.0 52.0 %shard_map.17 = f32[2,16,128]{2,1,0:T(8,128)} custom-call(f32[96,6,16,128]{3,2,1,0:T(8,128)} %bitcast.1), custom_call_target="tpu_custom_call" | custom-call | tf_op jit(solution)/shard_map/pallas_call | solution.py:264
  52.0 1.3 %copy.3 = f32[2,16,128]{2,1,0:T(8,128)} copy(f32[2,16,128]{2,1,0:T(8,128)} %shard_map.17) | data formatting | bytes 32768
